TPU v7x, 32 devices: a whole 2x2x4 slice. The times are simulated.
32 devices in a mesh: rep: 4 (over y, core), shard: 8 (over z, x).
Axes of the slice: x: 2, y: 2, z: 4, core: 2. Of those that a mesh axis runs over, the one named last changes fastest.
Arguments:
- hidden: bfloat16 [14336, 3584], P(('rep', 'shard')), may hold values from -144 to 144
- cotangent: bfloat16 [14336, 1024], P(('rep', 'shard')), may hold values from -6 to 6
- seq_ids: int32 [32, 448], P(('rep', 'shard')), may hold values from 0 to 3, as said below
- response_mask: int32 [32, 448], P(('rep', 'shard')), may hold values from 0 to 1, as said below
- group_ids: int32 [32, 4], P(('rep', 'shard')), may hold values from 0 to 15
- rewards: float32 [32, 4], P(('rep', 'shard')), may hold values from -6 to 6
- new_logp: float32 [32, 448], P(('rep', 'shard')), may hold values from -1.5 to -0.1
- old_logp: float32 [32, 448], P(('rep', 'shard')), may hold values from -1.5 to -0.1
- ref_logp: float32 [32, 448], P(('rep', 'shard')), may hold values from -1.5 to -0.1
- master: float32 [3, 3584, 1024], P(None, 'shard'), may hold values from -6 to 6
Outputs:
- new_master: float32 [3584, 1024], P('shard')
- rollout: bfloat16 [3, 3584, 2048], P(None, None, 'shard')
Inputs may be any that keep to these rules, and one draw needn't show every extreme that they name: `seq_ids`: each row numbers its device's 4 sequences in token order, never falling, each with one token or more. `response_mask`: within a sequence, prompt tokens come before response tokens; a sequence may have no response tokens.
All inputs are finite; a program needn't handle non-finite values.
Results may differ from a plain program's by a relative error of at most 0.0095.
Values may be sent and summed in bfloat16 or wider, within the bound.
A program may use at most 128 MiB of HBM per device.

v0:
```python
import jax
import jax.numpy as jnp
from jax import lax
from jax.sharding import PartitionSpec as P

HEAD = 128
KV_HEADS = 4
TP = 8
SEQ_DEV = 4


def token_coef(seq_row, mask_row, adv_row, new_row, old_row, ref_row):
    onehot = (seq_row[:, None] == jnp.arange(SEQ_DEV, dtype=jnp.int32)[None, :]).astype(jnp.float32)
    maskf = mask_row.astype(jnp.float32)
    lengths = jnp.maximum(jnp.dot(maskf, onehot, precision=lax.Precision.HIGHEST), 1.0)
    tok_len = jnp.dot(onehot, lengths, precision=lax.Precision.HIGHEST)
    tok_adv = jnp.dot(onehot, adv_row, precision=lax.Precision.HIGHEST)
    surrogate = -tok_adv * jnp.exp(new_row - old_row) + 0.2 * (1.0 - jnp.exp(ref_row - new_row))
    return maskf / tok_len * surrogate


def group_advantage(group_flat, reward_flat, stats):
    groups = stats.shape[1]
    onehot = (group_flat[:, None] == jnp.arange(groups, dtype=jnp.int32)[None, :]).astype(
        jnp.float32
    )
    count = jnp.maximum(stats[0], 1.0)
    mean = stats[1] / count
    spread = jnp.sqrt(jnp.maximum(stats[2] / count - mean * mean, 0.0))
    tok_mean = jnp.dot(onehot, mean, precision=lax.Precision.HIGHEST)
    tok_std = jnp.dot(onehot, jnp.maximum(spread, 0.5), precision=lax.Precision.HIGHEST)
    return (reward_flat - tok_mean) / tok_std


def group_sums(group_flat, reward_flat, groups):
    onehot = (group_flat[:, None] == jnp.arange(groups, dtype=jnp.int32)[None, :]).astype(
        jnp.float32
    )
    values = jnp.stack([jnp.ones_like(reward_flat), reward_flat, reward_flat * reward_flat], axis=0)
    return jnp.dot(values, onehot, precision=lax.Precision.HIGHEST)


def rounded(term):
    return lax.optimization_barrier(term.astype(jnp.bfloat16)).astype(jnp.float32)


def rollout_blocks(weights):
    layer_count = weights.shape[0]
    row_count = weights.shape[1]
    paired = weights.reshape(layer_count, row_count, 2, KV_HEADS, HEAD).transpose(0, 1, 3, 2, 4)
    paired = paired.reshape(layer_count, row_count, KV_HEADS, 2 * HEAD)
    by_rank = jnp.repeat(paired, TP // KV_HEADS, axis=2)
    copies = jnp.tile(by_rank, (1, 1, lax.axis_size("shard") // TP, 1))
    return copies.reshape(layer_count, row_count, lax.axis_size("shard") * 2 * HEAD)


def per_device(
    hidden,
    cotangent,
    seq_ids,
    response_mask,
    group_ids,
    rewards,
    new_logp,
    old_logp,
    ref_logp,
    master,
):
    n_rep = lax.axis_size("rep")
    n_shard = lax.axis_size("shard")
    groups = n_rep * n_shard * SEQ_DEV // 8
    rest_cols = lax.all_to_all(
        rollout_blocks(master[1:].astype(jnp.bfloat16)),
        "shard",
        split_axis=2,
        concat_axis=1,
        tiled=True,
    )
    local_sums = group_sums(group_ids[0], rewards[0], groups)
    stats = lax.psum(local_sums, ("rep", "shard"))
    advantage = group_advantage(group_ids[0], rewards[0], stats)
    coef = token_coef(
        seq_ids[0], response_mask[0], advantage, new_logp[0], old_logp[0], ref_logp[0]
    )
    delta = (coef[:, None] * cotangent.astype(jnp.float32)).astype(jnp.bfloat16)
    feature_count = hidden.shape[1]
    partial_value = lax.psum_scatter(
        rounded(
            lax.dot_general(
                hidden, delta, (((0,), (0,)), ((), ())), preferred_element_type=jnp.float32
            )
        ).astype(jnp.bfloat16),
        "shard",
        scatter_dimension=0,
        tiled=True,
    )
    grad = lax.psum(partial_value, "rep").astype(jnp.float32)
    squares = lax.psum(jnp.sum(grad * grad), "shard")
    rms = jnp.sqrt(squares / (feature_count * grad.shape[1]) + 1e-06)
    new_master = master[0] - 0.5 * grad / rms
    first_cols = lax.all_to_all(
        rollout_blocks(new_master[None].astype(jnp.bfloat16)),
        "shard",
        split_axis=2,
        concat_axis=1,
        tiled=True,
    )
    rollout = jnp.concatenate([first_cols, rest_cols], axis=0)
    return (new_master, rollout)


def solution(mesh):
    in_specs = (
        P(("rep", "shard"), None),
        P(("rep", "shard"), None),
        P(("rep", "shard"), None),
        P(("rep", "shard"), None),
        P(("rep", "shard"), None),
        P(("rep", "shard"), None),
        P(("rep", "shard"), None),
        P(("rep", "shard"), None),
        P(("rep", "shard"), None),
        P(None, "shard", None),
    )
    out_specs = (P("shard", None), P(None, None, "shard"))
    return jax.shard_map(
        per_device, mesh=mesh, in_specs=in_specs, out_specs=out_specs, check_vma=False
    )
```

profile of v0, /device:TPU:0, one launch (start us, length us, event | category | flops | bytes accessed | tf_op | source)
XLA Modules:
  0.0 468.4 jit_solution(8274017862780211825)
XLA Ops:
  7.2 0.0 reduce-scatter.4.cloned.1.call-start
  7.2 0.8 mul.39
  8.1 1.0 fusion.15
  9.0 41.9 %psum.21 = f32[3,16]{1,0:T(4,128)S(1)} all-reduce(f32[3,16]{1,0:T(4,128)S(1)} %fusion.15), channel_id=1, replica_groups=mesh['rep'=4,'shard'=8] {'rep','shard'}, use_global_device_ids=true, to_apply=%region_0.0 | all-reduce | flops 48 | bytes 384 | tf_op jit(solution)/shard_map/psum | solution.py:80
  51.0 0.8 convolution_bitcast_fusion
  51.8 0.9 fusion.8
  52.7 0.7 convert_element_type.31
  53.4 0.9 fusion.5
  54.3 1.0 fusion.10
  55.3 1.0 fusion.11
  56.3 0.8 subtract_exponential_fusion
  57.1 7.5 %fusion = bf16[3584,1024]{0,1:T(8,128)(2,1)} fusion(bf16[448,3584]{1,0:T(8,128)(2,1)S(1)} %copy-done, bf16[448,1024]{1,0:T(8,128)(2,1)} %param.11, f32[448]{0:T(512)S(1)} %add_multiply_fusion), kind=kOutput, calls=%fused_computation.1 | convolution fusion | flops 3293380608 | bytes 11470592 | tf_op jit(solution)/shard_map/dot_general | solution.py:89
  64.6 10.4 %copy.47 = bf16[3584,1024]{1,0:T(8,128)(2,1)} copy(bf16[3584,1024]{0,1:T(8,128)(2,1)} %fusion) | data formatting | bytes 14680064
  75.0 0.0 reduce-scatter.4.cloned.1.call-update
  75.0 2.3 slice.36
  77.4 2.3 reshape.41
  79.6 5.7 %copy.49 = bf16[2,448,2,4,128]{1,0,4,2,3:T(2,128)(2,1)S(1)} copy(bf16[2,448,2,4,128]{4,3,2,1,0:T(4,128)(2,1)} %reshape.41) | data formatting | bytes 3670016 | tf_op jit(solution)/shard_map/transpose | solution.py:50
  85.3 4.2 broadcast_in_dim.15
  89.5 5.3 %all-to-all-start.1 = ((bf16[2,448,2048]{1,0,2:T(2,128)(2,1)}), bf16[2,448,2048]{1,0,2:T(2,128)(2,1)}, u32[]{:S(2)}, u32[]{:S(2)}) async-start(bf16[2,448,2048]{1,0,2:T(2,128)(2,1)} %bitcast.83), calls=%async_computation.1 | async-start | bytes 8388608 | tf_op jit(solution)/shard_map/all_to_all | solution.py:72
  94.8 0.0 all-reduce.2.cloned.1.call-start
  94.9 188.3 %reduce-scatter.4.cloned.1.call-done = bf16[448,1024]{1,0:T(8,128)(2,1)} async-done(((bf16[3584,1024]{1,0:T(8,128)(2,1)}), bf16[448,1024]{1,0:T(8,128)(2,1)}) %reduce-scatter.4.cloned.1.call-update) | async-done | bytes 917520
  283.2 2.2 copy.48
  285.4 0.0 all-reduce.2.cloned.1.call-update
  285.4 36.1 %all-reduce.2.cloned.1.call-done = bf16[448,1024]{0,1:T(8,128)(2,1)} async-done(((bf16[448,1024]{0,1:T(8,128)(2,1)}), bf16[448,1024]{0,1:T(8,128)(2,1)}) %all-reduce.2.cloned.1.call-update) | async-done | bytes 917520 | tf_op jit(solution)/shard_map/psum | solution.py:97
  321.5 2.4 fusion.3
  323.9 1.9 copy.51
  325.7 22.1 %psum.23 = f32[]{:T(128)} all-reduce(f32[]{:T(128)} %fusion.3), channel_id=1, replica_groups=mesh['rep'=4,'shard'=8] {'shard'}, use_global_device_ids=true, to_apply=%region_4.0 | all-reduce | flops 1 | bytes 8 | tf_op jit(solution)/shard_map/psum | solution.py:98
  348.6 3.0 fusion.36
  351.6 3.6 copy.33
  355.2 2.7 reshape.40
  357.9 0.7 copy.34
  358.6 2.5 broadcast_in_dim.6
  361.1 5.3 %broadcast_in_dim.14 = bf16[1,448,2048]{2,1,0:T(8,128)(2,1)} reshape(bf16[448,4,2,256]{3,2,1,0:T(2,128)(2,1)} %broadcast_in_dim.6) | data formatting | bytes 3670016 | tf_op jit(solution)/shard_map/broadcast_in_dim | solution.py:52
  366.4 10.7 %copy.35 = bf16[1,448,2048]{1,0,2:T(2,128)(2,1)} copy(bf16[1,448,2048]{2,1,0:T(8,128)(2,1)} %broadcast_in_dim.14) | data formatting | bytes 3670016 | tf_op jit(solution)/shard_map/broadcast_in_dim | solution.py:52
  377.1 0.5 broadcast.50
  377.6 15.4 %reduce = bf16[2048,448]{1,0:T(8,128)(2,1)} reduce(bf16[2048,1,448]{2,1,0:T(2,128)(2,1)} %bitcast.84, bf16[]{:T(256)} %broadcast.50), dimensions={1}, to_apply=%bitcast.77.reduce_sub_computation | reduce | bytes 3670018
  393.1 6.8 %reshape.57 = bf16[8,2,57344]{2,1,0:T(2,128)(2,1)} reshape(bf16[2048,448]{1,0:T(8,128)(2,1)} %reduce) | data formatting | bytes 3670016
  399.8 4.3 all-to-all-start
  404.2 11.1 %copy.46 = bf16[2,448,8,256]{3,1,2,0:T(8,128)(2,1)} copy(bf16[2,448,8,256]{1,0,3,2:T(2,128)(2,1)} %bitcast.27) | data formatting | bytes 7340032 | tf_op jit(solution)/shard_map/all_to_all | solution.py:72
  415.3 1.7 copy.42
  417.0 25.9 %all-to-all-done = bf16[8,2,57344]{2,1,0:T(2,128)(2,1)} async-done(((bf16[8,2,57344]{2,1,0:T(2,128)(2,1)}), bf16[8,2,57344]{2,1,0:T(2,128)(2,1)}, u32[]{:S(2)}, u32[]{:S(2)}) %all-to-all-start) | async-done | bytes 1835040 | tf_op jit(solution)/shard_map/all_to_all | solution.py:101
  442.9 7.2 %reshape.58 = bf16[2048,1,448]{2,1,0:T(2,128)(2,1)} reshape(bf16[8,2,57344]{2,1,0:T(2,128)(2,1)} %all-to-all-done) | data formatting | bytes 3670016
  450.1 2.8 copy.50
  452.9 3.0 copy.43
  455.8 2.0 copy.37
  457.9 0.6 copy-done.2
  458.4 2.9 pad_maximum_fusion
  461.3 0.2 copy-done.1
  (12 shorter events, 0.0 us)
Async XLA Ops:
  7.2 49.9 %copy-start = (bf16[448,3584]{1,0:T(8,128)(2,1)S(1)}, bf16[448,3584]{1,0:T(8,128)(2,1)}, u32[]{:S(2)}) copy-start(bf16[448,3584]{1,0:T(8,128)(2,1)} %param.10) | copy-start | bytes 9633796
  7.2 276.0 %reduce-scatter.4.cloned.1.call-start = ((), (), s32[]{:S(2)}) async-start(), calls=%async_computation.4 | async-start | bytes 8257536
  89.5 310.4 %all-to-all-start.1 = ((bf16[2,448,2048]{1,0,2:T(2,128)(2,1)}), bf16[2,448,2048]{1,0,2:T(2,128)(2,1)}, u32[]{:S(2)}, u32[]{:S(2)}) async-start(bf16[2,448,2048]{1,0,2:T(2,128)(2,1)} %bitcast.83), calls=%async_computation.1 | async-start | bytes 8388608 | tf_op jit(solution)/shard_map/all_to_all | solution.py:72
  94.8 226.7 %all-reduce.2.cloned.1.call-start = ((), (), s32[]{:S(2)}) async-start(), calls=%async_computation.3 | async-start | bytes 2097152 | tf_op jit(solution)/shard_map/psum | solution.py:97
  285.4 38.5 %slice-start = ((f32[3,448,1024]{2,1,0:T(8,128)}), f32[1,448,1024]{2,1,0:T(8,128)S(1)}, s32[]{:S(2)}) async-start(f32[3,448,1024]{2,1,0:T(8,128)} %param.19), calls=%async_computation.5 | async-start | bytes 3670016 | tf_op jit(solution)/shard_map/slice | solution.py:100
  323.9 24.7 %copy-start.3 = (bf16[448,1024]{0,1:T(8,128)(2,1)S(1)}, bf16[448,1024]{0,1:T(8,128)(2,1)}, u32[]{:S(2)}) copy-start(bf16[448,1024]{0,1:T(8,128)(2,1)} %all-reduce.2.cloned.1.call-done) | copy-start | bytes 2752516
  399.8 43.1 %all-to-all-start = ((bf16[8,2,57344]{2,1,0:T(2,128)(2,1)}), bf16[8,2,57344]{2,1,0:T(2,128)(2,1)}, u32[]{:S(2)}, u32[]{:S(2)}) async-start(bf16[8,2,57344]{2,1,0:T(2,128)(2,1)} %reshape.57), calls=%async_computation | async-start | bytes 3670016 | tf_op jit(solution)/shard_map/all_to_all | solution.py:101
  455.8 2.6 copy-start.2
  458.4 3.1 copy-start.1
Sparse Core Ops, SparseCore 0:
  75.2 207.9 reduce-scatter.3
  286.1 35.3 all-reduce.1
where the time goes:
time: 470 us; the launch traced here: 468 us
  waiting for transfers between devices  250 us (53%)
  local copies, waits for them, and re-layouts  90.3 us (19%)
  blocking collectives  64.1 us (14%)
  other arithmetic  26 us (6%)
  between operations  14.8 us (3%)
  matrix products  13.1 us (3%)
  starting transfers between devices  9.74 us (2%)
    unnamed x3, waiting for transfers between devices  188 us
    psum x1, blocking collectives, per_device(): stats = lax.psum(local_sums, ('rep', 'shard'))  41.9 us
    psum x1, waiting for transfers between devices, per_device(): grad = lax.psum(partial_value, 'rep').astype(jnp.float32)  36.1 us
    unnamed x16, local copies, waits for them, and re-layouts  34.2 us
    all_to_all x1, waiting for transfers between devices, per_device(): lax.all_to_all(rollout_blocks(new_master[None].astype(jnp.bfloat16)), 'sh...  25.9 us
    broadcast_in_dim x4, local copies, waits for them, and re-layouts, rollout_blocks(): by_rank = jnp.repeat(paired, TP // KV_HEADS, axis=2)  22.7 us
    psum x1, blocking collectives, per_device(): squares = lax.psum(jnp.sum(grad * grad), 'shard')  22.1 us
    unnamed x1, other arithmetic  15.4 us
  transfers between devices with their start and end apart: 4, of which 3 were waited for; matrix products, arithmetic and copies ran while one was open for 18% of the time, Pallas kernels for 0%

commit v1 on v0

--- a/solution.py
+++ b/solution.py
@@ -7,6 +7,11 @@
 KV_HEADS = 4
 TP = 8
 SEQ_DEV = 4
+
+
+def update_array_now(u_in, axis_name):
+    m_next = jax.lax.all_gather(u_in, axis_name)
+    return jnp.sum(m_next, 0)
 
 
 def token_coef(seq_row, mask_row, adv_row, new_row, old_row, ref_row):
@@ -77,7 +82,7 @@
         tiled=True,
     )
     local_sums = group_sums(group_ids[0], rewards[0], groups)
-    stats = lax.psum(local_sums, ("rep", "shard"))
+    stats = update_array_now(local_sums, ("rep", "shard"))
     advantage = group_advantage(group_ids[0], rewards[0], stats)
     coef = token_coef(
         seq_ids[0], response_mask[0], advantage, new_logp[0], old_logp[0], ref_logp[0]

time: 470 us -> 495 us (1.053)
  blocking collectives: 64.1 us -> 92.2 us
    all_gather x0 -> x1, blocking collectives: none -> 70 us  [update_array_now(): m_next = jax.lax.all_gather(u_in, axis_name)]
    psum x1 -> x0, blocking collectives: 41.9 us -> none  [per_device(): stats = lax.psum(local_sums, ('rep', 'shard'))]
  transfers between devices with their start and end apart: 4 -> 4, of which waited for: 3 -> 3; matrix products, arithmetic and copies ran while one was open for 18% -> 17% of each run, Pallas kernels for 0% -> 0%
where the time goes in v1:
time: 495 us; the launch traced here: 493 us
  waiting for transfers between devices  248 us (50%)
  blocking collectives  92.2 us (19%)
  local copies, waits for them, and re-layouts  90.2 us (18%)
  other arithmetic  26.1 us (5%)
  between operations  14.8 us (3%)
  matrix products  13.1 us (3%)
  starting transfers between devices  8.93 us (2%)
    unnamed x3, waiting for transfers between devices  186 us
    all_gather x1, blocking collectives, update_array_now(): m_next = jax.lax.all_gather(u_in, axis_name)  70 us
    psum x1, waiting for transfers between devices, per_device(): grad = lax.psum(partial_value, 'rep').astype(jnp.float32)  36.1 us
    unnamed x16, local copies, waits for them, and re-layouts  34.2 us
    all_to_all x1, waiting for transfers between devices, per_device(): lax.all_to_all(rollout_blocks(new_master[None].astype(jnp.bfloat16)), 'sh...  25.9 us
    broadcast_in_dim x4, local copies, waits for them, and re-layouts, rollout_blocks(): by_rank = jnp.repeat(paired, TP // KV_HEADS, axis=2)  22.7 us
    psum x1, blocking collectives, per_device(): squares = lax.psum(jnp.sum(grad * grad), 'shard')  22.1 us
    unnamed x1, other arithmetic  15.4 us
  transfers between devices with their start and end apart: 4, of which 3 were waited for; matrix products, arithmetic and copies ran while one was open for 17% of the time, Pallas kernels for 0%

profile of v1, /device:TPU:0, one launch (start us, length us, event | category | flops | bytes accessed | tf_op | source)
XLA Modules:
  0.0 493.0 jit_solution(1659820713276005590)
XLA Ops:
  7.2 0.0 reduce-scatter.4.cloned.1.call-start
  7.2 0.8 mul.39
  8.1 1.0 convolution_bitcast_fusion
  9.0 70.0 %all-gather.1 = f32[32,3,16]{2,1,0:T(4,128)S(1)} all-gather(f32[1,3,16]{2,1,0:T(4,128)S(1)} %convolution_bitcast_fusion), channel_id=2, replica_groups=mesh['rep'=4,'shard'=8] {'rep','shard'}, dimensions={0}, use_global_device_ids=true | all-gather | bytes 6336 | tf_op jit(solution)/shard_map/all_gather | solution.py:13
  79.1 0.8 convolution_bitcast_fusion.1
  79.9 0.9 fusion.8
  80.8 0.7 convert_element_type.31
  81.5 0.9 fusion.5
  82.4 1.0 fusion.10
  83.4 1.0 fusion.11
  84.4 0.8 subtract_exponential_fusion
  85.2 7.5 %fusion = bf16[3584,1024]{0,1:T(8,128)(2,1)} fusion(bf16[448,3584]{1,0:T(8,128)(2,1)S(1)} %copy-done, bf16[448,1024]{1,0:T(8,128)(2,1)} %param.11, f32[448]{0:T(512)S(1)} %add_multiply_fusion), kind=kOutput, calls=%fused_computation.1 | convolution fusion | flops 3293380608 | bytes 11470592 | tf_op jit(solution)/shard_map/dot_general | solution.py:94
  92.7 10.4 %copy.47 = bf16[3584,1024]{1,0:T(8,128)(2,1)} copy(bf16[3584,1024]{0,1:T(8,128)(2,1)} %fusion) | data formatting | bytes 14680064
  103.1 0.0 reduce-scatter.4.cloned.1.call-update
  103.2 2.3 slice.36
  105.5 2.3 reshape.41
  107.8 5.6 %copy.49 = bf16[2,448,2,4,128]{1,0,4,2,3:T(2,128)(2,1)S(1)} copy(bf16[2,448,2,4,128]{4,3,2,1,0:T(4,128)(2,1)} %reshape.41) | data formatting | bytes 3670016 | tf_op jit(solution)/shard_map/transpose | solution.py:55
  113.4 4.2 broadcast_in_dim.15
  117.6 4.5 all-to-all-start.1
  122.1 0.0 all-reduce.2.cloned.1.call-start
  122.2 185.6 %reduce-scatter.4.cloned.1.call-done = bf16[448,1024]{1,0:T(8,128)(2,1)} async-done(((bf16[3584,1024]{1,0:T(8,128)(2,1)}), bf16[448,1024]{1,0:T(8,128)(2,1)}) %reduce-scatter.4.cloned.1.call-update) | async-done | bytes 917520
  307.8 2.2 copy.48
  310.0 0.0 all-reduce.2.cloned.1.call-update
  310.1 36.1 %all-reduce.2.cloned.1.call-done = bf16[448,1024]{0,1:T(8,128)(2,1)} async-done(((bf16[448,1024]{0,1:T(8,128)(2,1)}), bf16[448,1024]{0,1:T(8,128)(2,1)}) %all-reduce.2.cloned.1.call-update) | async-done | bytes 917520 | tf_op jit(solution)/shard_map/psum | solution.py:102
  346.1 2.4 fusion.3
  348.5 1.9 copy.51
  350.4 22.1 %psum.15 = f32[]{:T(128)} all-reduce(f32[]{:T(128)} %fusion.3), channel_id=1, replica_groups=mesh['rep'=4,'shard'=8] {'shard'}, use_global_device_ids=true, to_apply=%region_4.0 | all-reduce | flops 1 | bytes 8 | tf_op jit(solution)/shard_map/psum | solution.py:103
  373.2 3.0 fusion.35
  376.2 3.6 copy.33
  379.9 2.7 reshape.40
  382.5 0.7 copy.34
  383.2 2.5 broadcast_in_dim.6
  385.7 5.3 %broadcast_in_dim.14 = bf16[1,448,2048]{2,1,0:T(8,128)(2,1)} reshape(bf16[448,4,2,256]{3,2,1,0:T(2,128)(2,1)} %broadcast_in_dim.6) | data formatting | bytes 3670016 | tf_op jit(solution)/shard_map/broadcast_in_dim | solution.py:57
  391.0 10.7 %copy.35 = bf16[1,448,2048]{1,0,2:T(2,128)(2,1)} copy(bf16[1,448,2048]{2,1,0:T(8,128)(2,1)} %broadcast_in_dim.14) | data formatting | bytes 3670016 | tf_op jit(solution)/shard_map/broadcast_in_dim | solution.py:57
  401.8 0.5 broadcast.50
  402.3 15.4 %reduce.1 = bf16[2048,448]{1,0:T(8,128)(2,1)} reduce(bf16[2048,1,448]{2,1,0:T(2,128)(2,1)} %bitcast.86, bf16[]{:T(256)} %broadcast.50), dimensions={1}, to_apply=%bitcast.79.reduce_sub_computation | reduce | bytes 3670018
  417.7 6.8 %reshape.61 = bf16[8,2,57344]{2,1,0:T(2,128)(2,1)} reshape(bf16[2048,448]{1,0:T(8,128)(2,1)} %reduce.1) | data formatting | bytes 3670016
  424.5 4.3 all-to-all-start
  428.8 11.1 %copy.46 = bf16[2,448,8,256]{3,1,2,0:T(8,128)(2,1)} copy(bf16[2,448,8,256]{1,0,3,2:T(2,128)(2,1)} %bitcast.28) | data formatting | bytes 7340032 | tf_op jit(solution)/shard_map/all_to_all | solution.py:77
  439.9 1.7 copy.42
  441.7 25.9 %all-to-all-done = bf16[8,2,57344]{2,1,0:T(2,128)(2,1)} async-done(((bf16[8,2,57344]{2,1,0:T(2,128)(2,1)}), bf16[8,2,57344]{2,1,0:T(2,128)(2,1)}, u32[]{:S(2)}, u32[]{:S(2)}) %all-to-all-start) | async-done | bytes 1835040 | tf_op jit(solution)/shard_map/all_to_all | solution.py:106
  467.5 7.2 %reshape.62 = bf16[2048,1,448]{2,1,0:T(2,128)(2,1)} reshape(bf16[8,2,57344]{2,1,0:T(2,128)(2,1)} %all-to-all-done) | data formatting | bytes 3670016
  474.7 2.8 copy.50
  477.5 3.0 copy.43
  480.5 2.0 copy.37
  482.5 0.6 copy-done.2
  483.1 2.9 pad_maximum_fusion
  486.0 0.2 copy-done.1
  (13 shorter events, 0.1 us)
Async XLA Ops:
  7.2 78.1 %copy-start = (bf16[448,3584]{1,0:T(8,128)(2,1)S(1)}, bf16[448,3584]{1,0:T(8,128)(2,1)}, u32[]{:S(2)}) copy-start(bf16[448,3584]{1,0:T(8,128)(2,1)} %param.10) | copy-start | bytes 9633796
  7.2 300.6 %reduce-scatter.4.cloned.1.call-start = ((), (), s32[]{:S(2)}) async-start(), calls=%async_computation.4 | async-start | bytes 8257536
  117.6 306.9 %all-to-all-start.1 = ((bf16[2,448,2048]{1,0,2:T(2,128)(2,1)}), bf16[2,448,2048]{1,0,2:T(2,128)(2,1)}, u32[]{:S(2)}, u32[]{:S(2)}) async-start(bf16[2,448,2048]{1,0,2:T(2,128)(2,1)} %bitcast.85), calls=%async_computation.1 | async-start | bytes 8388608 | tf_op jit(solution)/shard_map/all_to_all | solution.py:77
  122.1 224.0 %all-reduce.2.cloned.1.call-start = ((), (), s32[]{:S(2)}) async-start(), calls=%async_computation.3 | async-start | bytes 2097152 | tf_op jit(solution)/shard_map/psum | solution.py:102
  310.0 38.5 %slice-start = ((f32[3,448,1024]{2,1,0:T(8,128)}), f32[1,448,1024]{2,1,0:T(8,128)S(1)}, s32[]{:S(2)}) async-start(f32[3,448,1024]{2,1,0:T(8,128)} %param.19), calls=%async_computation.5 | async-start | bytes 3670016 | tf_op jit(solution)/shard_map/slice | solution.py:105
  348.5 24.7 %copy-start.3 = (bf16[448,1024]{0,1:T(8,128)(2,1)S(1)}, bf16[448,1024]{0,1:T(8,128)(2,1)}, u32[]{:S(2)}) copy-start(bf16[448,1024]{0,1:T(8,128)(2,1)} %all-reduce.2.cloned.1.call-done) | copy-start | bytes 2752516
  424.5 43.1 %all-to-all-start = ((bf16[8,2,57344]{2,1,0:T(2,128)(2,1)}), bf16[8,2,57344]{2,1,0:T(2,128)(2,1)}, u32[]{:S(2)}, u32[]{:S(2)}) async-start(bf16[8,2,57344]{2,1,0:T(2,128)(2,1)} %reshape.61), calls=%async_computation | async-start | bytes 3670016 | tf_op jit(solution)/shard_map/all_to_all | solution.py:106
  480.5 2.6 copy-start.2
  483.1 3.1 copy-start.1
Sparse Core Ops, SparseCore 0:
  103.3 204.4 reduce-scatter.3
  310.7 35.3 all-reduce.1
